TPU v7x, 128 devices: a whole 4x4x4 slice. The times are simulated.
128 devices in a mesh: lat: 8 (over x, core), lon: 16 (over z, y).
Axes of the slice: x: 4, y: 4, z: 4, core: 2. Of those that a mesh axis runs over, the one named last changes fastest.
Arguments:
- tracers: bfloat16 [512, 2048, 32, 4], P('lat', 'lon'), may hold values from 0 to 2
- weights: bfloat16 [512, 16, 8, 128, 128], P('lat', 'lon'), may hold values from -1 to 1, as said below
- source_row: int32 [512, 16, 8], P('lat', 'lon'), may hold values from 0 to 511, as said below
- source_block: int32 [512, 16, 8], P('lat', 'lon'), may hold values from 0 to 15, as said below
- slot_count: int32 [512, 16], P('lat', 'lon'), may hold values from 1 to 8, as said below
Outputs:
- advected_fixed: float32 [512, 2048, 32, 4], P('lat', 'lon')
Inputs may be any that keep to these rules, and one draw needn't show every extreme that they name: source_row differs from the target tile's own row by at most 4 and lies within the grid. source_block lies at cyclic distance at most 2 from the target tile's own index along the row, except for target tiles of the first and the last latitude row, where it may reach 3; the allowed distance grows from 1 at the equator towards the poles; in the two outermost rows slot 0 reaches exactly 3 sectors ahead on even tiles and 3 sectors behind on odd tiles. slot_count grows from 1 or 2 at the equator to 8 at the two outermost rows. weights are of either sign; for each target tile the weights of each target cell over the used slots and all source cells sum (before rounding to bfloat16) to one value of that tile between 0.9 and 1.05.
All inputs are finite; a program needn't handle non-finite values.
Results may differ from a plain program's by a relative error of at most 0.0003.
Values may be sent and summed in bfloat16 or wider, within the bound.
No kernel may reach another device: no remote copies, remote signals or barrier semaphores. Data moves between devices by JAX's collectives and lax.ppermute only.
A program may use at most 192 MiB of HBM per device.

v0:
```python
import math
import jax
import jax.numpy as jnp
from jax import lax
from jax.sharding import Mesh
from jax.sharding import PartitionSpec as P

RLAT = 4
REACH = 3
LAT = ("lat_0", "lat_1")
LON = ("lon_0", "lon_1")
LAT_LON = ("lat_0", "lat_1", "lon_0", "lon_1")


def extended(value, sides, width):
    for axis, dim in sides:
        size, length = (lax.axis_size(axis), value.shape[dim])
        up = [(i, (i + 1) % size) for i in range(size - 1)]
        down = [(j, i) for i, j in up]
        last = lax.slice_in_dim(value, length - width, length, axis=dim)
        leading = lax.slice_in_dim(value, 0, width, axis=dim)
        before = lax.ppermute(last, axis, up)
        after = lax.ppermute(leading, axis, down)
        value = jnp.concatenate([before, value, after], axis=dim)
    return value


def shifted(value, axis, by):
    length = lax.axis_size(axis)
    return lax.ppermute(value, axis, [(i, (i + by) % length) for i in range(length)])


def by_axis(value, axes):
    for axis in axes:
        value = lax.psum(value, axis)
    return value


def latitude_area(total_rows, first_row, count_rows):
    rows_all = jnp.arange(count_rows, dtype=jnp.int32) + first_row
    angle = -0.5 * math.pi + (rows_all.astype(jnp.float32) + 0.5) * (math.pi / total_rows)
    return jnp.cos(angle)


def local(tracers, weights, source_row, source_block, slot_count):
    rows_dev, tile_width, levels, tracer_kinds = tracers.shape
    channels = levels * tracer_kinds
    lat_count = lax.axis_size(LAT)
    lon_count = lax.axis_size(LON)
    lat_index = lax.axis_index(LAT)
    lon_index = lax.axis_index(LON)
    field = tracers.reshape(rows_dev, tile_width, channels)
    total_rows = rows_dev * lat_count
    area = latitude_area(total_rows, lat_index * rows_dev, rows_dev)
    total_area = tile_width * lon_count * jnp.sum(latitude_area(total_rows, 0, total_rows))
    mass_old = jnp.sum(area[:, None, None] * field, axis=(0, 1))
    padded = extended(field, ((LAT, 0),), RLAT)
    local_row = source_row[:, 0, :] - (lat_index * rows_dev - RLAT)
    wanted = source_block[:, 0, :]
    slots_max = source_row.shape[2]
    relative = (wanted - lon_index + REACH) % lon_count - REACH
    near_list = []
    for distance in range(-(REACH - 1), REACH):
        if distance == 0:
            near_list.append(padded)
        else:
            near_list.append(shifted(padded, LON, -distance))
    near_stack = jnp.stack(near_list, axis=1)
    near_pick = near_stack[local_row, jnp.clip(relative + REACH - 1, 0, 2 * REACH - 2)]
    polar_slab = jnp.concatenate(
        [padded[RLAT : 2 * RLAT + 1], padded[rows_dev - 1 : rows_dev + RLAT]], axis=0
    )
    far_list = [shifted(polar_slab, LON, -distance) for distance in (-REACH, REACH)]
    upper = (jnp.arange(rows_dev, dtype=jnp.int32) < rows_dev // 2)[:, None]
    far_row = jnp.where(upper, local_row - RLAT, local_row - (rows_dev - 1) + RLAT + 1)
    far_row = jnp.clip(far_row, 0, 2 * RLAT + 1)
    far_stack = jnp.stack(far_list, axis=1)
    far_pick = far_stack[
        jnp.clip(far_row, 0, far_stack.shape[0] - 1), (relative > 0).astype(jnp.int32)
    ]
    active = jnp.arange(slots_max, dtype=jnp.int32)[None, :] < slot_count
    is_far = jnp.abs(relative) == REACH
    picked = jnp.where(
        (active & is_far)[:, :, None, None],
        far_pick,
        jnp.where(active[:, :, None, None], near_pick, jnp.zeros((), near_pick.dtype)),
    )
    advected = jnp.einsum(
        "tkij,tkjc->tic", weights[:, 0], picked, preferred_element_type=jnp.float32
    )
    mass_new = jnp.sum(area[:, None, None] * advected, axis=(0, 1))
    summed_old, summed_new = (by_axis(mass_old, LAT_LON), by_axis(mass_new, LAT_LON))
    fixed = advected + (summed_old - summed_new) / total_area
    return fixed.reshape(rows_dev, tile_width, levels, tracer_kinds)


def solution(mesh):
    finer = Mesh(mesh.devices.reshape(4, 2, 4, 4), ("lat_0", "lat_1", "lon_0", "lon_1"))
    placed = (
        P(LAT, LON, None, None),
        P(LAT, LON, None, None, None),
        P(LAT, LON, None),
        P(LAT, LON, None),
        P(LAT, LON),
    )
    return jax.shard_map(
        local, mesh=finer, in_specs=placed, out_specs=P(LAT, LON, None, None), check_vma=False
    )
```

profile of v0, /device:TPU:0, one launch (start us, length us, event | category | flops | bytes accessed | tf_op | source)
XLA Modules:
  0.0 289.7 jit_solution(14839024553744103163)
XLA Ops:
  0.0 0.0 copy-start
  0.0 1.2 fusion.28
  1.2 1.3 collective-permute-start.2
  2.5 1.3 collective-permute-start.3
  3.8 0.0 collective-permute-done.2
  3.8 3.8 %collective-permute-done.3 = bf16[4,128,128]{1,2,0:T(8,128)(2,1)S(1)} collective-permute-done((bf16[4,128,128]{1,2,0:T(8,128)(2,1)S(1)}, bf16[4,128,128]{1,2,0:T(8,128)(2,1)S(1)}, u32[]{:S(2)}, u32[]{:S(2)}) %collective-permute-start.3) | collective-permute-done | bytes 131104 | tf_op jit(solution)/shard_map/ppermute | solution.py:23
  7.6 3.3 %pad_maximum_fusion = bf16[72,128,128]{1,2,0:T(8,128)(2,1)} fusion(bf16[4,128,128]{1,2,0:T(8,128)(2,1)S(1)} %collective-permute-done.3, bf16[64,128,128]{1,2,0:T(8,128)(2,1)} %bitcast.64, bf16[4,128,128]{1,2,0:T(8,128)(2,1)S(1)} %collective-permute-done.2), kind=kLoop, calls=%fused_computation.13 | loop fusion | flops 2359296 | bytes 4718592 | tf_op jit(solution)/shard_map/concatenate | solution.py:24
  10.9 3.2 %collective-permute-start.4 = (bf16[72,128,128]{1,2,0:T(8,128)(2,1)}, bf16[72,128,128]{1,2,0:T(8,128)(2,1)}, u32[]{:S(2)}, u32[]{:S(2)}) collective-permute-start(bf16[72,128,128]{1,2,0:T(8,128)(2,1)} %pad_maximum_fusion), channel_id=1, source_target_pairs={{0,2},{1,3},{2,4},{3,5},{4,6},{5,7},{6,8},{7,9},{8,10},{9,11},{10,... | collective-permute-start | bytes 7077896 | tf_op jit(solution)/shard_map/ppermute | solution.py:30
  14.1 0.7 collective-permute-start.5
  14.8 4.7 %collective-permute-start.6 = (bf16[72,128,128]{1,2,0:T(8,128)(2,1)}, bf16[72,128,128]{1,2,0:T(8,128)(2,1)}, u32[]{:S(2)}, u32[]{:S(2)}) collective-permute-start(bf16[72,128,128]{1,2,0:T(8,128)(2,1)} %pad_maximum_fusion), channel_id=1, source_target_pairs={{0,15},{1,0},{2,1},{3,2},{4,3},{5,4},{6,5},{7,6},{8,7},{9,8},{10,9... | collective-permute-start | bytes 7077896 | tf_op jit(solution)/shard_map/ppermute | solution.py:30
  19.4 0.0 copy-done
  19.4 0.1 fusion.29
  19.6 0.9 collective-permute-start.7
  20.6 0.1 collective-permute-start
  20.7 0.0 copy-done.2
  20.7 0.0 copy-done.4
  20.7 0.0 copy-done.3
  20.7 155.5 %collective-permute-done = bf16[10,128,128]{1,2,0:T(8,128)(2,1)S(1)} collective-permute-done((bf16[10,128,128]{1,2,0:T(8,128)(2,1)S(1)}, bf16[10,128,128]{1,2,0:T(8,128)(2,1)S(1)}, u32[]{:S(2)}, u32[]{:S(2)}) %collective-permute-start) | collective-permute-done | bytes 327712 | tf_op jit(solution)/shard_map/ppermute | solution.py:30
  176.2 4.5 %collective-permute-start.1 = (bf16[10,128,128]{1,2,0:T(8,128)(2,1)S(1)}, bf16[10,128,128]{1,2,0:T(8,128)(2,1)S(1)}, u32[]{:S(2)}, u32[]{:S(2)}) collective-permute-start(bf16[10,128,128]{1,2,0:T(8,128)(2,1)S(1)} %pad_maximum_fusion.2), channel_id=1, source_target_pairs={{0,13},{1,14},{2,15},{3,0},{4,1},{5,2},{6,3},{7,4},{8,5},{9,6},{10... | collective-permute-start | bytes 983048 | tf_op jit(solution)/shard_map/ppermute | solution.py:30
  180.8 0.1 copy.11
  180.9 0.1 reshape.258
  181.0 0.1 copy.9
  181.0 0.1 reshape.252
  181.1 0.1 copy.10
  181.2 0.1 copy.8
  181.3 1.4 multiply_reduce_fusion
  182.7 0.1 reduce_sum.30
  182.8 0.7 cosine_reduce_fusion
  184.1 3.8 %collective-permute-done.1 = bf16[10,128,128]{1,2,0:T(8,128)(2,1)S(1)} collective-permute-done((bf16[10,128,128]{1,2,0:T(8,128)(2,1)S(1)}, bf16[10,128,128]{1,2,0:T(8,128)(2,1)S(1)}, u32[]{:S(2)}, u32[]{:S(2)}) %collective-permute-start.1) | collective-permute-done | bytes 327712 | tf_op jit(solution)/shard_map/ppermute | solution.py:30
  188.0 0.7 copy-done.1
  188.7 1.0 pad_maximum_fusion.1
  189.7 10.8 %gather_fusion = bf16[512,128,128]{1,2,0:T(8,128)(2,1)} fusion(bf16[10,2,128,128]{2,3,0,1:T(8,128)(2,1)S(1)} %pad_maximum_fusion.1, s32[512]{0:T(512)S(1)} %reshape.252), kind=kCustom, calls=%fused_computation | custom fusion | bytes 33558528 | tf_op jit(solution)/shard_map/gather | solution.py:78
  200.5 0.0 collective-permute-done.4
  200.5 3.3 %bitcast_dynamic-update-slice_fusion.4 = bf16[72,5,128,128]{2,3,0,1:T(8,128)(2,1)} fusion(bf16[72,128,128]{1,2,0:T(8,128)(2,1)} %collective-permute-done.4), kind=kLoop, calls=%fused_computation.18 | loop fusion | bytes 4718592
  203.9 0.0 collective-permute-done.5
  203.9 3.4 %bitcast_dynamic-update-slice_fusion.3 = bf16[72,5,128,128]{2,3,0,1:T(8,128)(2,1)} fusion(bf16[72,5,128,128]{2,3,0,1:T(8,128)(2,1)} %bitcast_dynamic-update-slice_fusion.4, bf16[72,128,128]{1,2,0:T(8,128)(2,1)} %collective-permute-done.5), kind=kLoop, calls=%fused_computation.17 | loop fusion | bytes 4718592
  207.3 1.6 bitcast_dynamic-update-slice_fusion.2
  208.8 0.0 collective-permute-done.6
  208.8 3.4 %bitcast_dynamic-update-slice_fusion.1 = bf16[72,5,128,128]{2,3,0,1:T(8,128)(2,1)} fusion(bf16[72,5,128,128]{2,3,0,1:T(8,128)(2,1)} %bitcast_dynamic-update-slice_fusion.2, bf16[72,128,128]{1,2,0:T(8,128)(2,1)} %collective-permute-done.6), kind=kLoop, calls=%fused_computation.15 | loop fusion | bytes 4718592
  212.2 0.0 collective-permute-done.7
  212.2 3.4 %bitcast_dynamic-update-slice_fusion = bf16[72,5,128,128]{2,3,0,1:T(8,128)(2,1)} fusion(bf16[72,5,128,128]{2,3,0,1:T(8,128)(2,1)} %bitcast_dynamic-update-slice_fusion.1, bf16[72,128,128]{1,2,0:T(8,128)(2,1)} %collective-permute-done.7), kind=kLoop, calls=%fused_computation.14 | loop fusion | bytes 4718592 | tf_op jit(solution)/shard_map/stack | solution.py:68
  215.6 15.2 %gather_fusion.1 = bf16[512,128,128]{1,2,0:T(8,128)(2,1)} fusion(bf16[72,5,128,128]{2,3,0,1:T(8,128)(2,1)} %bitcast_dynamic-update-slice_fusion, s32[512]{0:T(512)S(1)} %reshape.258), kind=kCustom, calls=%fused_computation.1 | custom fusion | bytes 33558528 | tf_op jit(solution)/shard_map/gather | solution.py:69
  230.7 19.4 %fusion.7 = (f32[128]{0:T(128)S(1)}, f32[64,128,128,1]{2,1,3,0:T(8,128)}) fusion(f32[64]{0:T(128)S(1)} %add_cosine_fusion, bf16[64,1,8,128,128]{4,3,2,1,0:T(8,128)(2,1)} %param.6, bf16[64,8,128,128]{2,3,1,0:T(8,128)(2,1)} %bitcast.66, bf16[64,8,128,128]{2,3,1,0:T(8,128)(2,1)} %bitcast.67, pred[64,8]{1,0:T(8,128)(4,1)S(1)} %copy.10, pred[64,8]{1,0:T(8,128)(4,1)S(1)} %copy.8), kind=kOutput, calls=%fused_computation.11 | convolution fusion | flops 2166358016 | bytes 54527744 | tf_op jit(solution)/shard_map/tkij,tkjc->tic/dot_general | solution.py:88
  250.2 12.5 %all-reduce.2 = (f32[128]{0:T(128)S(1)}, f32[128]{0:T(128)S(1)}) all-reduce(f32[128]{0:T(128)S(1)} %reduce_sum.30, f32[128]{0:T(128)S(1)} %get-tuple-element.21), channel_id=1, replica_groups=mesh['lat_0'=4,'lat_1'=2,'lon_0'=4,'lon_1'=4] {'lat_0'}, use_global_device_ids=true, to_apply=%region_1.0 | all-reduce | flops 256 | bytes 2048 | tf_op jit(solution)/shard_map/psum | solution.py:35
  262.6 2.5 all-reduce.3
  265.1 8.2 %all-reduce.1 = (f32[128]{0:T(128)S(1)}, f32[128]{0:T(128)S(1)}) all-reduce(f32[128]{0:T(128)S(1)} %get-tuple-element.11, f32[128]{0:T(128)S(1)} %get-tuple-element.12), channel_id=1, replica_groups=mesh['lat_0'=4,'lat_1'=2,'lon_0'=4,'lon_1'=4] {'lon_0'}, use_global_device_ids=true, to_apply=%region_3.4 | all-reduce | flops 256 | bytes 2048 | tf_op jit(solution)/shard_map/psum | solution.py:35
  273.3 11.6 %all-reduce = (f32[128]{0:T(128)S(1)}, f32[128]{0:T(128)S(1)}) all-reduce(f32[128]{0:T(128)S(1)} %get-tuple-element.7, f32[128]{0:T(128)S(1)} %get-tuple-element.8), channel_id=1, replica_groups=mesh['lat_0'=4,'lat_1'=2,'lon_0'=4,'lon_1'=4] {'lon_1'}, use_global_device_ids=true, to_apply=%region_4.5 | all-reduce | flops 256 | bytes 2048 | tf_op jit(solution)/shard_map/psum | solution.py:35
  284.8 4.9 %bitcast_add_fusion = f32[64,128,128]{2,1,0:T(8,128)} fusion(f32[64,128,128,1]{2,1,3,0:T(8,128)} %get-tuple-element.22, f32[128]{0:T(128)S(1)} %subtract_divide_fusion), kind=kLoop, calls=%fused_computation.9 | loop fusion | flops 1048576 | bytes 8389120 | tf_op jit(solution)/shard_map/add | solution.py:93
  (10 shorter events, 0.1 us)
Async XLA Ops:
  0.0 19.4 %copy-start = (bf16[64,128,32,4]{1,3,2,0:T(4,128)(2,1)S(1)}, bf16[64,128,32,4]{1,3,2,0:T(4,128)(2,1)}, u32[]{:S(2)}) copy-start(bf16[64,128,32,4]{1,3,2,0:T(4,128)(2,1)} %param.5) | copy-start | bytes 6291460
  0.0 20.7 %copy-start.2 = (s32[64,1,8]{0,2,1:T(8,128)S(1)}, s32[64,1,8]{0,2,1:T(8,128)}, u32[]{:S(2)}) copy-start(s32[64,1,8]{0,2,1:T(8,128)} %param.8) | copy-start | bytes 6148
  0.0 20.7 %copy-start.4 = (s32[64,1]{0,1:T(1,128)S(1)}, s32[64,1]{0,1:T(1,128)}, u32[]{:S(2)}) copy-start(s32[64,1]{0,1:T(1,128)} %param.9) | copy-start | bytes 772
  0.0 20.7 %copy-start.3 = (s32[64,1,8]{0,2,1:T(8,128)S(1)}, s32[64,1,8]{0,2,1:T(8,128)}, u32[]{:S(2)}) copy-start(s32[64,1,8]{0,2,1:T(8,128)} %param.7) | copy-start | bytes 6148
  1.2 2.6 collective-permute-start.2
  2.5 5.1 %collective-permute-start.3 = (bf16[4,128,128]{1,2,0:T(8,128)(2,1)S(1)}, bf16[4,128,128]{1,2,0:T(8,128)(2,1)S(1)}, u32[]{:S(2)}, u32[]{:S(2)}) collective-permute-start(bf16[4,128,128]{1,2,0:T(8,128)(2,1)S(1)} %bitcast.72), channel_id=1, source_target_pairs={{16,0},{32,16},{48,32},{64,48},{80,64},{96,80},{112,96},{17,1},{33... | collective-permute-start | bytes 393224 | tf_op jit(solution)/shard_map/ppermute | solution.py:23
  10.9 189.6 %collective-permute-start.4 = (bf16[72,128,128]{1,2,0:T(8,128)(2,1)}, bf16[72,128,128]{1,2,0:T(8,128)(2,1)}, u32[]{:S(2)}, u32[]{:S(2)}) collective-permute-start(bf16[72,128,128]{1,2,0:T(8,128)(2,1)} %pad_maximum_fusion), channel_id=1, source_target_pairs={{0,2},{1,3},{2,4},{3,5},{4,6},{5,7},{6,8},{7,9},{8,10},{9,11},{10,... | collective-permute-start | bytes 7077896 | tf_op jit(solution)/shard_map/ppermute | solution.py:30
  14.1 189.8 %collective-permute-start.5 = (bf16[72,128,128]{1,2,0:T(8,128)(2,1)}, bf16[72,128,128]{1,2,0:T(8,128)(2,1)}, u32[]{:S(2)}, u32[]{:S(2)}) collective-permute-start(bf16[72,128,128]{1,2,0:T(8,128)(2,1)} %pad_maximum_fusion), channel_id=1, source_target_pairs={{0,1},{1,2},{2,3},{3,4},{4,5},{5,6},{6,7},{7,8},{8,9},{9,10},{10,1... | collective-permute-start | bytes 7077896 | tf_op jit(solution)/shard_map/ppermute | solution.py:30
  14.8 194.1 %collective-permute-start.6 = (bf16[72,128,128]{1,2,0:T(8,128)(2,1)}, bf16[72,128,128]{1,2,0:T(8,128)(2,1)}, u32[]{:S(2)}, u32[]{:S(2)}) collective-permute-start(bf16[72,128,128]{1,2,0:T(8,128)(2,1)} %pad_maximum_fusion), channel_id=1, source_target_pairs={{0,15},{1,0},{2,1},{3,2},{4,3},{5,4},{6,5},{7,6},{8,7},{9,8},{10,9... | collective-permute-start | bytes 7077896 | tf_op jit(solution)/shard_map/ppermute | solution.py:30
  19.6 192.6 %collective-permute-start.7 = (bf16[72,128,128]{1,2,0:T(8,128)(2,1)}, bf16[72,128,128]{1,2,0:T(8,128)(2,1)}, u32[]{:S(2)}, u32[]{:S(2)}) collective-permute-start(bf16[72,128,128]{1,2,0:T(8,128)(2,1)} %pad_maximum_fusion), channel_id=1, source_target_pairs={{0,14},{1,15},{2,0},{3,1},{4,2},{5,3},{6,4},{7,5},{8,6},{9,7},{10,... | collective-permute-start | bytes 7077896 | tf_op jit(solution)/shard_map/ppermute | solution.py:30
  20.6 155.7 %collective-permute-start = (bf16[10,128,128]{1,2,0:T(8,128)(2,1)S(1)}, bf16[10,128,128]{1,2,0:T(8,128)(2,1)S(1)}, u32[]{:S(2)}, u32[]{:S(2)}) collective-permute-start(bf16[10,128,128]{1,2,0:T(8,128)(2,1)S(1)} %pad_maximum_fusion.2), channel_id=1, source_target_pairs={{0,3},{1,4},{2,5},{3,6},{4,7},{5,8},{6,9},{7,10},{8,11},{9,12},{10... | collective-permute-start | bytes 983048 | tf_op jit(solution)/shard_map/ppermute | solution.py:30
  176.2 11.8 %collective-permute-start.1 = (bf16[10,128,128]{1,2,0:T(8,128)(2,1)S(1)}, bf16[10,128,128]{1,2,0:T(8,128)(2,1)S(1)}, u32[]{:S(2)}, u32[]{:S(2)}) collective-permute-start(bf16[10,128,128]{1,2,0:T(8,128)(2,1)S(1)} %pad_maximum_fusion.2), channel_id=1, source_target_pairs={{0,13},{1,14},{2,15},{3,0},{4,1},{5,2},{6,3},{7,4},{8,5},{9,6},{10... | collective-permute-start | bytes 983048 | tf_op jit(solution)/shard_map/ppermute | solution.py:30
  188.0 0.7 copy-start.1
where the time goes:
time: 290 us
  waiting for transfers between devices  163 us (56%)
  local copies, waits for them, and re-layouts  42.2 us (15%)
  blocking collectives  34.6 us (12%)
  matrix products  19.4 us (7%)
  starting transfers between devices  16.7 us (6%)
  other arithmetic  13 us (4%)
    ppermute x6, waiting for transfers between devices, shifted(): lax.ppermute(value, axis, [(i, (i + by) % length) for i in range(length)])  159 us
    psum x4, blocking collectives, by_axis(): value = lax.psum(value, axis)  34.6 us
    dot_general x1, matrix products, local(): jnp.einsum('tkij,tkjc->tic', weights[:, 0], picked, preferred_element_typ...  19.4 us
    gather x1, local copies, waits for them, and re-layouts, local(): near_stack[local_row, jnp.clip(relative + REACH - 1, 0, 2 * REACH - 2)]  15.2 us
    ppermute x6, starting transfers between devices, shifted(): lax.ppermute(value, axis, [(i, (i + by) % length) for i in range(length)])  14.1 us
    unnamed x13, local copies, waits for them, and re-layouts  10.9 us
    gather x1, local copies, waits for them, and re-layouts, local(): far_stack[jnp.clip(far_row, 0, far_stack.shape[0] - 1), (relative > 0).as...  10.8 us
  transfers between devices with their start and end apart: 8, of which 3 were waited for; matrix products, arithmetic and copies ran while one was open for 9% of the time, Pallas kernels for 0%

commit v1 on v0

--- a/solution.py
+++ b/solution.py
@@ -10,6 +10,12 @@
 LAT = ("lat_0", "lat_1")
 LON = ("lon_0", "lon_1")
 LAT_LON = ("lat_0", "lat_1", "lon_0", "lon_1")
+
+
+def add_all(x, axis):
+    parts = lax.all_gather(x, axis, axis=0, tiled=False)
+    result = parts.sum(axis=0)
+    return result
 
 
 def extended(value, sides, width):
@@ -32,7 +38,7 @@
 
 def by_axis(value, axes):
     for axis in axes:
-        value = lax.psum(value, axis)
+        value = add_all(value, axis)
     return value
 
 

time: 290 us -> 306 us (1.055)
  blocking collectives: 34.6 us -> 53.7 us
  waiting for transfers between devices: 163 us -> 159 us
    all_gather x0 -> x8, blocking collectives: none -> 53.7 us  [add_all(): parts = lax.all_gather(x, axis, axis=0, tiled=False)]
    psum x4 -> x0, blocking collectives: 34.6 us -> none  [by_axis(): value = lax.psum(value, axis)]
    ppermute x6, waiting for transfers between devices: 159 us -> 155 us  [shifted(): lax.ppermute(value, axis, [(i, (i + by) % length) for i in range(length)])]
    unnamed x13 -> x14, local copies, waits for them, and re-layouts: 10.9 us -> 11 us
  transfers between devices with their start and end apart: 8 -> 8, of which waited for: 3 -> 2; matrix products, arithmetic and copies ran while one was open for 9% -> 9% of each run, Pallas kernels for 0% -> 0%
where the time goes in v1:
time: 306 us; the launch traced here: 305 us
  waiting for transfers between devices  159 us (52%)
  blocking collectives  53.7 us (18%)
  local copies, waits for them, and re-layouts  42.2 us (14%)
  matrix products  19.4 us (6%)
  starting transfers between devices  16.7 us (5%)
  other arithmetic  13.3 us (4%)
    ppermute x6, waiting for transfers between devices, shifted(): lax.ppermute(value, axis, [(i, (i + by) % length) for i in range(length)])  155 us
    all_gather x8, blocking collectives, add_all(): parts = lax.all_gather(x, axis, axis=0, tiled=False)  53.7 us
    dot_general x1, matrix products, local(): jnp.einsum('tkij,tkjc->tic', weights[:, 0], picked, preferred_element_typ...  19.4 us
    gather x1, local copies, waits for them, and re-layouts, local(): near_stack[local_row, jnp.clip(relative + REACH - 1, 0, 2 * REACH - 2)]  15.2 us
    ppermute x6, starting transfers between devices, shifted(): lax.ppermute(value, axis, [(i, (i + by) % length) for i in range(length)])  14.1 us
    unnamed x14, local copies, waits for them, and re-layouts  11 us
    gather x1, local copies, waits for them, and re-layouts, local(): far_stack[jnp.clip(far_row, 0, far_stack.shape[0] - 1), (relative > 0).as...  10.8 us
  transfers between devices with their start and end apart: 8, of which 2 were waited for; matrix products, arithmetic and copies ran while one was open for 9% of the time, Pallas kernels for 0%

profile of v1, /device:TPU:0, one launch (start us, length us, event | category | flops | bytes accessed | tf_op | source)
XLA Modules:
  0.0 305.4 jit_solution(10397597126511674741)
XLA Ops:
  0.0 1.2 fusion.28
  1.2 1.3 collective-permute-start.2
  2.5 1.3 collective-permute-start.3
  3.8 0.0 collective-permute-done.2
  3.8 3.8 %collective-permute-done.3 = bf16[4,128,128]{1,2,0:T(8,128)(2,1)S(1)} collective-permute-done((bf16[4,128,128]{1,2,0:T(8,128)(2,1)S(1)}, bf16[4,128,128]{1,2,0:T(8,128)(2,1)S(1)}, u32[]{:S(2)}, u32[]{:S(2)}) %collective-permute-start.3) | collective-permute-done | bytes 131104 | tf_op jit(solution)/shard_map/ppermute | solution.py:29
  7.6 3.3 %pad_maximum_fusion = bf16[72,128,128]{1,2,0:T(8,128)(2,1)} fusion(bf16[4,128,128]{1,2,0:T(8,128)(2,1)S(1)} %collective-permute-done.3, bf16[64,128,128]{1,2,0:T(8,128)(2,1)} %bitcast.71, bf16[4,128,128]{1,2,0:T(8,128)(2,1)S(1)} %collective-permute-done.2), kind=kLoop, calls=%fused_computation.13 | loop fusion | flops 2359296 | bytes 4718592 | tf_op jit(solution)/shard_map/concatenate | solution.py:30
  10.9 3.2 %collective-permute-start.4 = (bf16[72,128,128]{1,2,0:T(8,128)(2,1)}, bf16[72,128,128]{1,2,0:T(8,128)(2,1)}, u32[]{:S(2)}, u32[]{:S(2)}) collective-permute-start(bf16[72,128,128]{1,2,0:T(8,128)(2,1)} %pad_maximum_fusion), channel_id=1, source_target_pairs={{0,2},{1,3},{2,4},{3,5},{4,6},{5,7},{6,8},{7,9},{8,10},{9,11},{10,... | collective-permute-start | bytes 7077896 | tf_op jit(solution)/shard_map/ppermute | solution.py:36
  14.1 0.7 collective-permute-start.5
  14.8 4.7 %collective-permute-start.6 = (bf16[72,128,128]{1,2,0:T(8,128)(2,1)}, bf16[72,128,128]{1,2,0:T(8,128)(2,1)}, u32[]{:S(2)}, u32[]{:S(2)}) collective-permute-start(bf16[72,128,128]{1,2,0:T(8,128)(2,1)} %pad_maximum_fusion), channel_id=1, source_target_pairs={{0,15},{1,0},{2,1},{3,2},{4,3},{5,4},{6,5},{7,6},{8,7},{9,8},{10,9... | collective-permute-start | bytes 7077896 | tf_op jit(solution)/shard_map/ppermute | solution.py:36
  19.4 0.0 copy-done
  19.4 0.1 fusion.29
  19.6 0.9 collective-permute-start.7
  20.6 0.1 collective-permute-start
  20.7 155.5 %collective-permute-done = bf16[10,128,128]{1,2,0:T(8,128)(2,1)S(1)} collective-permute-done((bf16[10,128,128]{1,2,0:T(8,128)(2,1)S(1)}, bf16[10,128,128]{1,2,0:T(8,128)(2,1)S(1)}, u32[]{:S(2)}, u32[]{:S(2)}) %collective-permute-start) | collective-permute-done | bytes 327712 | tf_op jit(solution)/shard_map/ppermute | solution.py:36
  176.2 4.5 %collective-permute-start.1 = (bf16[10,128,128]{1,2,0:T(8,128)(2,1)S(1)}, bf16[10,128,128]{1,2,0:T(8,128)(2,1)S(1)}, u32[]{:S(2)}, u32[]{:S(2)}) collective-permute-start(bf16[10,128,128]{1,2,0:T(8,128)(2,1)S(1)} %pad_maximum_fusion.2), channel_id=1, source_target_pairs={{0,13},{1,14},{2,15},{3,0},{4,1},{5,2},{6,3},{7,4},{8,5},{9,6},{10... | collective-permute-start | bytes 983048 | tf_op jit(solution)/shard_map/ppermute | solution.py:36
  180.8 0.1 copy.15
  180.9 0.1 reshape.264
  181.0 0.1 copy.13
  181.0 0.1 reshape.258
  181.1 0.1 copy.12
  181.2 0.1 copy.14
  181.3 1.4 multiply_reduce_fusion
  182.7 0.1 reshape.277
  182.8 10.3 %all-gather.7 = f32[4,1,128]{2,1,0:T(1,128)S(1)} all-gather(f32[1,1,128]{2,1,0:T(1,128)S(1)} %reshape.277), channel_id=1, replica_groups=mesh['lat_0'=4,'lat_1'=2,'lon_0'=4,'lon_1'=4] {'lat_0'}, dimensions={0}, use_global_device_ids=true | all-gather | bytes 2560 | tf_op jit(solution)/shard_map/all_gather | solution.py:16
  193.2 1.8 all-gather.8
  195.0 7.4 %all-gather.9 = f32[4,1,128]{2,1,0:T(1,128)S(1)} all-gather(f32[1,1,128]{2,1,0:T(1,128)S(1)} %bitcast.81), channel_id=3, replica_groups=mesh['lat_0'=4,'lat_1'=2,'lon_0'=4,'lon_1'=4] {'lon_0'}, dimensions={0}, use_global_device_ids=true | all-gather | bytes 2560 | tf_op jit(solution)/shard_map/all_gather | solution.py:16
  202.4 7.7 %all-gather.10 = f32[4,1,128]{2,1,0:T(1,128)S(1)} all-gather(f32[1,1,128]{2,1,0:T(1,128)S(1)} %bitcast.82), channel_id=4, replica_groups=mesh['lat_0'=4,'lat_1'=2,'lon_0'=4,'lon_1'=4] {'lon_1'}, dimensions={0}, use_global_device_ids=true | all-gather | bytes 2560 | tf_op jit(solution)/shard_map/all_gather | solution.py:16
  210.1 0.7 cosine_reduce_fusion
  211.5 0.0 collective-permute-done.1
  211.5 0.7 copy-done.1
  212.2 1.0 pad_maximum_fusion.1
  213.3 10.8 %gather_fusion = bf16[512,128,128]{1,2,0:T(8,128)(2,1)} fusion(bf16[10,2,128,128]{2,3,0,1:T(8,128)(2,1)S(1)} %pad_maximum_fusion.1, s32[512]{0:T(512)S(1)} %reshape.258), kind=kCustom, calls=%fused_computation | custom fusion | bytes 33558528 | tf_op jit(solution)/shard_map/gather | solution.py:84
  224.1 0.0 collective-permute-done.4
  224.1 3.3 %bitcast_dynamic-update-slice_fusion.4 = bf16[72,5,128,128]{2,3,0,1:T(8,128)(2,1)} fusion(bf16[72,128,128]{1,2,0:T(8,128)(2,1)} %collective-permute-done.4), kind=kLoop, calls=%fused_computation.18 | loop fusion | bytes 4718592
  227.4 0.0 collective-permute-done.5
  227.4 3.4 %bitcast_dynamic-update-slice_fusion.3 = bf16[72,5,128,128]{2,3,0,1:T(8,128)(2,1)} fusion(bf16[72,5,128,128]{2,3,0,1:T(8,128)(2,1)} %bitcast_dynamic-update-slice_fusion.4, bf16[72,128,128]{1,2,0:T(8,128)(2,1)} %collective-permute-done.5), kind=kLoop, calls=%fused_computation.17 | loop fusion | bytes 4718592
  230.8 1.7 bitcast_dynamic-update-slice_fusion.2
  232.5 0.0 collective-permute-done.6
  232.5 3.4 %bitcast_dynamic-update-slice_fusion.1 = bf16[72,5,128,128]{2,3,0,1:T(8,128)(2,1)} fusion(bf16[72,5,128,128]{2,3,0,1:T(8,128)(2,1)} %bitcast_dynamic-update-slice_fusion.2, bf16[72,128,128]{1,2,0:T(8,128)(2,1)} %collective-permute-done.6), kind=kLoop, calls=%fused_computation.15 | loop fusion | bytes 4718592
  235.9 0.0 collective-permute-done.7
  235.9 3.4 %bitcast_dynamic-update-slice_fusion = bf16[72,5,128,128]{2,3,0,1:T(8,128)(2,1)} fusion(bf16[72,5,128,128]{2,3,0,1:T(8,128)(2,1)} %bitcast_dynamic-update-slice_fusion.1, bf16[72,128,128]{1,2,0:T(8,128)(2,1)} %collective-permute-done.7), kind=kLoop, calls=%fused_computation.14 | loop fusion | bytes 4718592 | tf_op jit(solution)/shard_map/stack | solution.py:74
  239.3 15.2 %gather_fusion.1 = bf16[512,128,128]{1,2,0:T(8,128)(2,1)} fusion(bf16[72,5,128,128]{2,3,0,1:T(8,128)(2,1)} %bitcast_dynamic-update-slice_fusion, s32[512]{0:T(512)S(1)} %reshape.264), kind=kCustom, calls=%fused_computation.1 | custom fusion | bytes 33558528 | tf_op jit(solution)/shard_map/gather | solution.py:75
  254.5 19.4 %fusion.7 = (f32[128]{0:T(128)S(1)}, f32[64,128,128,1]{2,1,3,0:T(8,128)}) fusion(f32[64]{0:T(128)S(1)} %add_cosine_fusion, bf16[64,1,8,128,128]{4,3,2,1,0:T(8,128)(2,1)} %param.6, bf16[64,8,128,128]{2,3,1,0:T(8,128)(2,1)} %bitcast.73, bf16[64,8,128,128]{2,3,1,0:T(8,128)(2,1)} %bitcast.74, pred[64,8]{1,0:T(8,128)(4,1)S(1)} %copy.14, pred[64,8]{1,0:T(8,128)(4,1)S(1)} %copy.12), kind=kOutput, calls=%fused_computation.11 | convolution fusion | flops 2166358016 | bytes 54527744 | tf_op jit(solution)/shard_map/tkij,tkjc->tic/dot_general | solution.py:94
  273.9 7.9 %all-gather.11 = f32[4,1,128]{2,1,0:T(1,128)S(1)} all-gather(f32[1,1,128]{2,1,0:T(1,128)S(1)} %bitcast.86), channel_id=5, replica_groups=mesh['lat_0'=4,'lat_1'=2,'lon_0'=4,'lon_1'=4] {'lat_0'}, dimensions={0}, use_global_device_ids=true | all-gather | bytes 2560 | tf_op jit(solution)/shard_map/all_gather | solution.py:16
  281.8 1.8 all-gather.12
  283.6 8.6 %all-gather.13 = f32[4,1,128]{2,1,0:T(1,128)S(1)} all-gather(f32[1,1,128]{2,1,0:T(1,128)S(1)} %bitcast.83), channel_id=7, replica_groups=mesh['lat_0'=4,'lat_1'=2,'lon_0'=4,'lon_1'=4] {'lon_0'}, dimensions={0}, use_global_device_ids=true | all-gather | bytes 2560 | tf_op jit(solution)/shard_map/all_gather | solution.py:16
  292.2 8.3 %all-gather.14 = f32[4,1,128]{2,1,0:T(1,128)S(1)} all-gather(f32[1,1,128]{2,1,0:T(1,128)S(1)} %bitcast.84), channel_id=8, replica_groups=mesh['lat_0'=4,'lat_1'=2,'lon_0'=4,'lon_1'=4] {'lon_1'}, dimensions={0}, use_global_device_ids=true | all-gather | bytes 2560 | tf_op jit(solution)/shard_map/all_gather | solution.py:16
  300.5 4.9 %bitcast_add_fusion = f32[64,128,128]{2,1,0:T(8,128)} fusion(f32[64,128,128,1]{2,1,3,0:T(8,128)} %get-tuple-element.14, f32[128]{0:T(128)S(1)} %subtract_divide_fusion), kind=kLoop, calls=%fused_computation.9 | loop fusion | flops 1048576 | bytes 8389120 | tf_op jit(solution)/shard_map/add | solution.py:99
  (22 shorter events, 0.3 us)
Async XLA Ops:
  0.0 19.4 %copy-start = (bf16[64,128,32,4]{1,3,2,0:T(4,128)(2,1)S(1)}, bf16[64,128,32,4]{1,3,2,0:T(4,128)(2,1)}, u32[]{:S(2)}) copy-start(bf16[64,128,32,4]{1,3,2,0:T(4,128)(2,1)} %param.5) | copy-start | bytes 6291460
  0.0 20.7 %copy-start.2 = (s32[64,1,8]{0,2,1:T(8,128)S(1)}, s32[64,1,8]{0,2,1:T(8,128)}, u32[]{:S(2)}) copy-start(s32[64,1,8]{0,2,1:T(8,128)} %param.8) | copy-start | bytes 6148
  0.0 20.7 %copy-start.4 = (s32[64,1]{0,1:T(1,128)S(1)}, s32[64,1]{0,1:T(1,128)}, u32[]{:S(2)}) copy-start(s32[64,1]{0,1:T(1,128)} %param.9) | copy-start | bytes 772
  0.0 20.7 %copy-start.3 = (s32[64,1,8]{0,2,1:T(8,128)S(1)}, s32[64,1,8]{0,2,1:T(8,128)}, u32[]{:S(2)}) copy-start(s32[64,1,8]{0,2,1:T(8,128)} %param.7) | copy-start | bytes 6148
  1.2 2.6 collective-permute-start.2
  2.5 5.1 %collective-permute-start.3 = (bf16[4,128,128]{1,2,0:T(8,128)(2,1)S(1)}, bf16[4,128,128]{1,2,0:T(8,128)(2,1)S(1)}, u32[]{:S(2)}, u32[]{:S(2)}) collective-permute-start(bf16[4,128,128]{1,2,0:T(8,128)(2,1)S(1)} %bitcast.79), channel_id=1, source_target_pairs={{16,0},{32,16},{48,32},{64,48},{80,64},{96,80},{112,96},{17,1},{33... | collective-permute-start | bytes 393224 | tf_op jit(solution)/shard_map/ppermute | solution.py:29
  10.9 213.2 %collective-permute-start.4 = (bf16[72,128,128]{1,2,0:T(8,128)(2,1)}, bf16[72,128,128]{1,2,0:T(8,128)(2,1)}, u32[]{:S(2)}, u32[]{:S(2)}) collective-permute-start(bf16[72,128,128]{1,2,0:T(8,128)(2,1)} %pad_maximum_fusion), channel_id=1, source_target_pairs={{0,2},{1,3},{2,4},{3,5},{4,6},{5,7},{6,8},{7,9},{8,10},{9,11},{10,... | collective-permute-start | bytes 7077896 | tf_op jit(solution)/shard_map/ppermute | solution.py:36
  14.1 213.3 %collective-permute-start.5 = (bf16[72,128,128]{1,2,0:T(8,128)(2,1)}, bf16[72,128,128]{1,2,0:T(8,128)(2,1)}, u32[]{:S(2)}, u32[]{:S(2)}) collective-permute-start(bf16[72,128,128]{1,2,0:T(8,128)(2,1)} %pad_maximum_fusion), channel_id=1, source_target_pairs={{0,1},{1,2},{2,3},{3,4},{4,5},{5,6},{6,7},{7,8},{8,9},{9,10},{10,1... | collective-permute-start | bytes 7077896 | tf_op jit(solution)/shard_map/ppermute | solution.py:36
  14.8 217.8 %collective-permute-start.6 = (bf16[72,128,128]{1,2,0:T(8,128)(2,1)}, bf16[72,128,128]{1,2,0:T(8,128)(2,1)}, u32[]{:S(2)}, u32[]{:S(2)}) collective-permute-start(bf16[72,128,128]{1,2,0:T(8,128)(2,1)} %pad_maximum_fusion), channel_id=1, source_target_pairs={{0,15},{1,0},{2,1},{3,2},{4,3},{5,4},{6,5},{7,6},{8,7},{9,8},{10,9... | collective-permute-start | bytes 7077896 | tf_op jit(solution)/shard_map/ppermute | solution.py:36
  19.6 216.3 %collective-permute-start.7 = (bf16[72,128,128]{1,2,0:T(8,128)(2,1)}, bf16[72,128,128]{1,2,0:T(8,128)(2,1)}, u32[]{:S(2)}, u32[]{:S(2)}) collective-permute-start(bf16[72,128,128]{1,2,0:T(8,128)(2,1)} %pad_maximum_fusion), channel_id=1, source_target_pairs={{0,14},{1,15},{2,0},{3,1},{4,2},{5,3},{6,4},{7,5},{8,6},{9,7},{10,... | collective-permute-start | bytes 7077896 | tf_op jit(solution)/shard_map/ppermute | solution.py:36
  20.6 155.7 %collective-permute-start = (bf16[10,128,128]{1,2,0:T(8,128)(2,1)S(1)}, bf16[10,128,128]{1,2,0:T(8,128)(2,1)S(1)}, u32[]{:S(2)}, u32[]{:S(2)}) collective-permute-start(bf16[10,128,128]{1,2,0:T(8,128)(2,1)S(1)} %pad_maximum_fusion.2), channel_id=1, source_target_pairs={{0,3},{1,4},{2,5},{3,6},{4,7},{5,8},{6,9},{7,10},{8,11},{9,12},{10... | collective-permute-start | bytes 983048 | tf_op jit(solution)/shard_map/ppermute | solution.py:36
  176.2 35.3 %collective-permute-start.1 = (bf16[10,128,128]{1,2,0:T(8,128)(2,1)S(1)}, bf16[10,128,128]{1,2,0:T(8,128)(2,1)S(1)}, u32[]{:S(2)}, u32[]{:S(2)}) collective-permute-start(bf16[10,128,128]{1,2,0:T(8,128)(2,1)S(1)} %pad_maximum_fusion.2), channel_id=1, source_target_pairs={{0,13},{1,14},{2,15},{3,0},{4,1},{5,2},{6,3},{7,4},{8,5},{9,6},{10... | collective-permute-start | bytes 983048 | tf_op jit(solution)/shard_map/ppermute | solution.py:36
  211.5 0.7 copy-start.1
